TPU v7x, 32 devices: a whole 2x2x4 slice. The times are simulated.
32 devices in a mesh: row: 8 (over z, x), col: 4 (over y, core).
Axes of the slice: x: 2, y: 2, z: 4, core: 2. Of those that a mesh axis runs over, the one named last changes fastest.
Arguments:
- voltage: float32 [2, 4096, 16384], P(None, ('row', 'col')), may hold values from -6 to 6
- chirp_phase: float32 [16384, 4096], P(('row', 'col')), may hold values from -3.140625 to 3.140625
- filter_taps: float32 [8, 1024], replicated, may hold values from -0.0625 to 0.0625
Outputs:
- filterbank: float32 [2, 1024, 65536], P(None, None, ('row', 'col'))
All inputs are finite; a program needn't handle non-finite values.
Results may differ from a plain program's by a relative error of at most 0.00015.
Values sent between devices are 32-bit elements; how exact they have to be, the bound alone decides.
No kernel may reach another device: no remote copies, remote signals or barrier semaphores. Data moves between devices by JAX's collectives and lax.ppermute only.
A program may use at most 192 MiB of HBM per device.

v0:
```python
import math
import jax
import jax.numpy as jnp
from jax import lax
from jax.sharding import PartitionSpec as P

precise = lax.Precision.HIGHEST


def passed_along(block, axis, distance):
    devices = range(lax.axis_size(axis))
    route = [(i - distance, i) for i in devices if i - distance in devices]
    return lax.ppermute(block, axis, route)


def dft_table(radix, direction):
    digits = jnp.arange(radix, dtype=jnp.int32)
    product = digits[:, None] * digits[None, :] % radix
    turn = direction * 2.0 * math.pi / radix * product.astype(jnp.float32)
    cos_part = jnp.cos(turn)
    sin_part = jnp.sin(turn)
    upper = jnp.stack([cos_part, sin_part], axis=1)
    lower = jnp.stack([-sin_part, cos_part], axis=1)
    return jnp.stack([upper, lower], axis=0)


def complex_product(values, cos_part, sin_part):
    real_part = values[0] * cos_part - values[1] * sin_part
    imag_part = values[0] * sin_part + values[1] * cos_part
    return jnp.stack([real_part, imag_part])


def inner_twist(outer_radix, inner_radix, direction):
    outer_digits = jnp.arange(outer_radix, dtype=jnp.int32)
    inner_digits = jnp.arange(inner_radix, dtype=jnp.int32)
    length = outer_radix * inner_radix
    product = outer_digits[:, None] * inner_digits[None, :] % length
    turn = direction * 2.0 * math.pi / length * product.astype(jnp.float32)
    return (jnp.cos(turn), jnp.sin(turn))


def dft_rows(values, direction):
    length = values.shape[1]
    column_count = values.shape[2]
    inner_radix = min(length, 128)
    outer_radix = length // inner_radix
    blocked = values.reshape(2, outer_radix, inner_radix, column_count)
    partial_value = jnp.einsum(
        "cadk,cabm->dkbm", dft_table(outer_radix, direction), blocked, precision=precise
    )
    cos_part, sin_part = inner_twist(outer_radix, inner_radix, direction)
    partial_value = complex_product(partial_value, cos_part[:, :, None], sin_part[:, :, None])
    result = jnp.einsum(
        "cbdq,ckbm->dqkm", dft_table(inner_radix, direction), partial_value, precision=precise
    )
    return result.reshape(2, length, column_count)


def dft_cols(values, direction):
    length = values.shape[2]
    row_count = values.shape[1]
    inner_radix = min(length, 128)
    outer_radix = length // inner_radix
    blocked = values.reshape(2, row_count, outer_radix, inner_radix)
    partial_value = jnp.einsum(
        "cadk,cmab->dmkb", dft_table(outer_radix, direction), blocked, precision=precise
    )
    cos_part, sin_part = inner_twist(outer_radix, inner_radix, direction)
    partial_value = complex_product(partial_value, cos_part, sin_part)
    result = jnp.einsum(
        "cbdq,cmkb->dmqk", dft_table(inner_radix, direction), partial_value, precision=precise
    )
    return result.reshape(2, row_count, length)


def rotate(values, row_index, col_index, total, direction, factor):
    product = row_index[:, None] * col_index[None, :] % total
    turn = direction * 2.0 * math.pi / total * product.astype(jnp.float32)
    return complex_product(values, factor * jnp.cos(turn), factor * jnp.sin(turn))


def spread(values):
    return lax.all_to_all(values, ("row", "col"), split_axis=2, concat_axis=1, tiled=True)


def collect(values):
    return lax.all_to_all(values, ("row", "col"), split_axis=1, concat_axis=2, tiled=True)


def local(voltage, chirp_phase, filter_taps):
    device_count = lax.axis_size("row") * lax.axis_size("col")
    device = lax.axis_index(("row", "col"))
    local_rows = voltage.shape[1]
    total_rows = local_rows * device_count
    total_cols = voltage.shape[2]
    local_cols = total_cols // device_count
    total = total_rows * total_cols
    signal = spread(voltage)
    signal = dft_rows(signal, -1.0)
    row_index = jnp.arange(total_rows, dtype=jnp.int32)
    col_index = device * local_cols + jnp.arange(local_cols, dtype=jnp.int32)
    signal = rotate(signal, row_index, col_index, total, -1.0, 1.0)
    signal = collect(signal)
    signal = dft_cols(signal, -1.0)
    turned_phase = jnp.transpose(chirp_phase)
    local_phase = lax.all_to_all(
        turned_phase, ("row", "col"), split_axis=0, concat_axis=1, tiled=True
    )
    signal = complex_product(signal, jnp.cos(local_phase), jnp.sin(local_phase))
    signal = dft_cols(signal, 1.0)
    row_index = device * local_rows + jnp.arange(local_rows, dtype=jnp.int32)
    col_index = jnp.arange(total_cols, dtype=jnp.int32)
    signal = rotate(signal, row_index, col_index, total, 1.0, 1.0 / total)
    signal = spread(signal)
    signal = dft_rows(signal, 1.0)
    signal = collect(signal)
    tap_count = filter_taps.shape[0]
    channel_count = filter_taps.shape[1]
    samples = signal.reshape(2, local_rows * total_cols)
    frame_count = samples.shape[1] // channel_count
    frames = samples.reshape(2, frame_count, channel_count)
    history = passed_along(frames[:, frame_count - tap_count + 1 :, :], ("row", "col"), 1)
    extended = jnp.concatenate([history, frames], axis=1)
    turned = jnp.transpose(extended, (0, 2, 1))
    weighted = jnp.zeros((2, channel_count, frame_count), jnp.float32)
    for tap_delay in range(tap_count):
        offset = tap_count - 1 - tap_delay
        weighted = (
            weighted
            + filter_taps[tap_delay][None, :, None] * turned[:, :, offset : offset + frame_count]
        )
    return dft_rows(weighted, -1.0)


def solution(mesh):
    in_specs = (P(None, ("row", "col"), None), P(("row", "col"), None), P())
    out_specs = P(None, None, ("row", "col"))
    return jax.shard_map(local, mesh=mesh, in_specs=in_specs, out_specs=out_specs, check_vma=False)
```

profile of v0, /device:TPU:6, one launch (start us, length us, event | category | flops | bytes accessed | tf_op | source)
XLA Modules:
  0.0 2393.4 jit_solution(8709069159866349502)
XLA Ops:
  0.0 24.9 %copy.169 = f32[2,128,16384]{1,0,2:T(2,128)} copy(f32[2,128,16384]{2,1,0:T(8,128)} %param.3) | data formatting | bytes 33554432 | tf_op args[0]
  24.9 6.1 all-to-all-start
  31.0 9.1 copy.181
  40.1 370.0 %all-to-all-done = f32[2,128,16384]{1,0,2:T(2,128)} async-done(((f32[2,128,16384]{1,0,2:T(2,128)}), f32[2,128,16384]{1,0,2:T(2,128)}, u32[]{:S(2)}, u32[]{:S(2)}) %all-to-all-start) | async-done | bytes 16777248 | tf_op jit(solution)/shard_map/all_to_all | solution.py:83
  410.1 3.4 all-to-all-start.2
  414.6 20.2 copy.234
  434.8 21.7 fusion.71
  456.5 7.0 multiply_subtract_fusion.5
  463.5 3.3 pad_maximum_fusion
  466.8 28.9 %fusion.59 = f32[2,128,32,512]{3,1,2,0:T(8,128)S(1)} fusion(f32[2,32,128,512]{3,1,2,0:T(8,128)S(1)} %pad_maximum_fusion, f32[1,128,2,128]{1,3,0,2:T(8,128)S(1)} %get-tuple-element.30, f32[1,128,2,128]{1,3,0,2:T(8,128)S(1)} %get-tuple-element.29), kind=kOutput, calls=%fused_computation.103 | convolution fusion | flops 12884967424 | bytes 33816576 | tf_op jit(solution)/shard_map/cbdq,ckbm->dqkm/dot_general | solution.py:53
  495.7 7.0 fusion.139
  502.7 8.2 copy.172
  511.0 8.2 copy.173
  519.2 36.9 %fusion.51 = (f32[1,4096,512]{2,1,0:T(8,128)S(1)}, f32[1,4096,512]{2,1,0:T(8,128)S(1)}) fusion(f32[1,128,32,512]{3,2,1,0:T(8,128)S(1)} %copy.173, f32[1,128,32,512]{3,2,1,0:T(8,128)S(1)} %copy.172, s32[512]{0:T(512)S(1)} %iota_add_fusion), kind=kLoop, calls=%fused_computation.77 | loop fusion | flops 41943040 | bytes 33556480 | tf_op jit(solution)/shard_map/sub | solution.py:28
  556.1 1.8 pad_maximum_fusion.1
  557.9 32.2 %copy.174 = f32[2,4096,512]{2,0,1:T(2,128)} copy(f32[2,4096,512]{2,1,0:T(8,128)S(1)} %pad_maximum_fusion.1) | data formatting | bytes 33554432 | tf_op jit(solution)/shard_map/stack | solution.py:30
  590.2 11.6 all-to-all-done.2
  601.7 5.0 all-to-all-start.1
  607.9 31.5 %sine_bitcast_fusion = (f32[128,32,512]{2,0,1:T(8,128)}, f32[128,32,512]{2,0,1:T(8,128)}) fusion(f32[32,128,512]{2,1,0:T(8,128)} %all-to-all-done.2), kind=kLoop, calls=%fused_computation.93 | loop fusion | bytes 25165824 | tf_op jit(solution)/shard_map/sin | solution.py:109
  639.4 9.0 copy.182
  648.4 9.4 copy.183
  657.8 8.9 copy.184
  666.7 9.4 copy.185
  676.1 309.5 %all-to-all-done.1 = f32[2,4096,512]{2,0,1:T(2,128)} async-done(((f32[2,4096,512]{2,0,1:T(2,128)}), f32[2,4096,512]{2,0,1:T(2,128)}, u32[]{:S(2)}, u32[]{:S(2)}) %all-to-all-start.1) | async-done | bytes 16777248 | tf_op jit(solution)/shard_map/all_to_all | solution.py:87
  985.5 14.2 copy.175
  999.7 17.5 copy.176
  1017.2 18.1 copy.211
  1035.3 17.1 convolution_bitcast_fusion
  1052.4 7.0 multiply_subtract_fusion.4
  1059.4 31.5 %fusion.36 = f32[2,128,128,128]{2,3,0,1:T(8,128)} fusion(f32[1,128,128,128]{2,3,0,1:T(8,128)} %get-tuple-element.14, f32[1,128,128,128]{2,3,0,1:T(8,128)} %get-tuple-element.13, f32[1,128,2,128]{1,3,0,2:T(8,128)S(1)} %get-tuple-element.30, f32[1,128,2,128]{1,3,0,2:T(8,128)S(1)} %get-tuple-element.29), kind=kOutput, calls=%fused_computation.59 | convolution fusion | flops 12889161728 | bytes 33816576 | tf_op jit(solution)/shard_map/cbdq,cmkb->dmqk/dot_general | solution.py:70
  1090.9 19.0 multiply_subtract_fusion.3
  1109.8 17.3 fusion.37
  1127.2 7.1 multiply_subtract_fusion.2
  1134.3 31.7 %fusion.40 = f32[2,128,128,128]{2,3,0,1:T(8,128)S(1)} fusion(f32[1,128,128,128]{2,3,0,1:T(8,128)} %get-tuple-element.12, f32[1,128,128,128]{2,3,0,1:T(8,128)} %get-tuple-element.11, f32[1,128,2,128]{1,3,2,0:T(8,128)S(1)} %get-tuple-element.28, f32[1,128,2,128]{1,3,2,0:T(8,128)S(1)} %get-tuple-element.27), kind=kOutput, calls=%fused_computation.61 | convolution fusion | flops 12889161728 | bytes 33816576 | tf_op jit(solution)/shard_map/cbdq,cmkb->dmqk/dot_general | solution.py:70
  1166.0 6.8 fusion.138
  1172.8 9.4 copy.191
  1182.2 9.3 copy.192
  1191.5 36.6 %fusion.49 = (f32[1,128,16384]{1,2,0:T(8,128)S(1)}, f32[1,128,16384]{1,2,0:T(8,128)S(1)}) fusion(f32[1,128,128,128]{1,3,2,0:T(8,128)} %copy.192, f32[1,128,128,128]{1,3,2,0:T(8,128)} %copy.191, s32[128]{0:T(128)S(1)} %iota_add_fusion.1), kind=kLoop, calls=%fused_computation.71 | loop fusion | flops 46137344 | bytes 33554944 | tf_op jit(solution)/shard_map/sub | solution.py:28
  1228.1 1.2 pad_maximum_fusion.2
  1229.2 61.7 %copy.193 = f32[2,128,16384]{1,0,2:T(2,128)} copy(f32[2,128,16384]{1,2,0:T(8,128)S(1)} %pad_maximum_fusion.2) | data formatting | bytes 33554432 | tf_op jit(solution)/shard_map/stack | solution.py:30
  1291.0 4.0 all-to-all-start.3
  1295.5 377.9 %all-to-all-done.3 = f32[2,128,16384]{1,0,2:T(2,128)} async-done(((f32[2,128,16384]{1,0,2:T(2,128)}), f32[2,128,16384]{1,0,2:T(2,128)}, u32[]{:S(2)}, u32[]{:S(2)}) %all-to-all-start.3) | async-done | bytes 16777248 | tf_op jit(solution)/shard_map/all_to_all | solution.py:83
  1673.4 20.1 copy.247
  1693.4 21.7 fusion.74
  1715.2 7.0 multiply_subtract_fusion.1
  1722.2 3.3 pad_maximum_fusion.3
  1725.4 28.9 %fusion.62 = f32[2,128,32,512]{3,1,2,0:T(8,128)S(1)} fusion(f32[2,32,128,512]{3,1,2,0:T(8,128)S(1)} %pad_maximum_fusion.3, f32[1,128,2,128]{1,3,2,0:T(8,128)S(1)} %get-tuple-element.28, f32[1,128,2,128]{1,3,2,0:T(8,128)S(1)} %get-tuple-element.27), kind=kOutput, calls=%fused_computation.104 | convolution fusion | flops 12884967424 | bytes 33816576 | tf_op jit(solution)/shard_map/cbdq,ckbm->dqkm/dot_general | solution.py:53
  1754.3 20.1 copy.198
  1774.4 28.6 %copy.199 = f32[2,4096,512]{2,0,1:T(2,128)} copy(f32[2,4096,512]{2,1,0:T(8,128)} %bitcast.229) | data formatting | bytes 33554432 | tf_op jit(solution)/shard_map/reshape | solution.py:56
  1803.0 3.8 all-to-all-start.4
  1807.3 377.8 %all-to-all-done.4 = f32[2,4096,512]{2,0,1:T(2,128)} async-done(((f32[2,4096,512]{2,0,1:T(2,128)}), f32[2,4096,512]{2,0,1:T(2,128)}, u32[]{:S(2)}, u32[]{:S(2)}) %all-to-all-start.4) | async-done | bytes 16777248 | tf_op jit(solution)/shard_map/all_to_all | solution.py:87
  2185.1 17.8 copy.279
  2202.9 19.2 reshape_reshape.3
  2222.1 0.8 slice.168
  2222.9 1.9 collective-permute-start
  2225.0 3.5 collective-permute-done
  2228.5 11.8 maximum_bitcast_fusion
  2240.3 50.0 %fusion = f32[2,1024,2048]{1,2,0:T(8,128)} fusion(f32[2,1024,2055]{1,2,0:T(8,128)} %maximum_bitcast_fusion, f32[1024]{0:T(1024)S(1)} %bitcast.241, f32[1024]{0:T(1024)S(1)} %bitcast.242, f32[1024]{0:T(1024)S(1)} %bitcast.236, f32[1024]{0:T(1024)S(1)} %bitcast.237, f32[1024]{0:T(1024)S(1)} %bitcast.238, f32[1024]{0:T(1024)S(1)} %bitcast.239, ...), kind=kLoop, calls=%fused_computation.2 | loop fusion | flops 62914560 | bytes 151027712 | tf_op jit(solution)/shard_map/add | solution.py:129
  2290.3 17.3 copy.201
  2307.7 32.0 %fusion.65 = f32[2,8,128,2048]{3,1,2,0:T(8,128)} fusion(f32[2,8,128,2048]{3,2,1,0:T(8,128)} %bitcast.231, f32[1,8,2,8]{1,3,0,2:T(8,128)S(1)} %copy.167, f32[1,8,2,8]{1,3,0,2:T(8,128)S(1)} %copy.166), kind=kOutput, calls=%fused_computation.105 | convolution fusion | flops 805306624 | bytes 33555456 | tf_op jit(solution)/shard_map/cadk,cabm->dkbm/dot_general | solution.py:48
  2339.7 7.2 multiply_subtract_fusion
  2347.0 2.0 pad_maximum_fusion.4
  2349.0 23.7 fusion.68
  2372.7 20.2 copy.278
  (38 shorter events, 3.2 us)
Async XLA Ops:
  24.9 385.2 %all-to-all-start = ((f32[2,128,16384]{1,0,2:T(2,128)}), f32[2,128,16384]{1,0,2:T(2,128)}, u32[]{:S(2)}, u32[]{:S(2)}) async-start(f32[2,128,16384]{1,0,2:T(2,128)} %copy.169), calls=%async_computation | async-start | bytes 33554432 | tf_op jit(solution)/shard_map/all_to_all | solution.py:83
  410.1 191.6 %all-to-all-start.2 = ((f32[32,128,512]{2,1,0:T(8,128)}), f32[32,128,512]{2,1,0:T(8,128)}, u32[]{:S(2)}, u32[]{:S(2)}) async-start(f32[32,128,512]{2,1,0:T(8,128)} %bitcast.232), calls=%async_computation.2 | async-start | bytes 16777216 | tf_op jit(solution)/shard_map/all_to_all | solution.py:106
  414.6 644.8 %copy-start = (f32[1,128,2,128]{1,3,0,2:T(8,128)}, f32[1,128,2,128]{1,3,0,2:T(8,128)S(1)}, u32[]{:S(2)}) copy-start(f32[1,128,2,128]{1,3,0,2:T(8,128)S(1)} %get-tuple-element.29) | copy-start | bytes 393220
  414.6 644.8 %copy-start.2 = (f32[1,128,2,128]{1,3,0,2:T(8,128)}, f32[1,128,2,128]{1,3,0,2:T(8,128)S(1)}, u32[]{:S(2)}) copy-start(f32[1,128,2,128]{1,3,0,2:T(8,128)S(1)} %get-tuple-element.30) | copy-start | bytes 393220
  601.7 383.8 %all-to-all-start.1 = ((f32[2,4096,512]{2,0,1:T(2,128)}), f32[2,4096,512]{2,0,1:T(2,128)}, u32[]{:S(2)}, u32[]{:S(2)}) async-start(f32[2,4096,512]{2,0,1:T(2,128)} %copy.174), calls=%async_computation.1 | async-start | bytes 33554432 | tf_op jit(solution)/shard_map/all_to_all | solution.py:87
  1291.0 382.4 %all-to-all-start.3 = ((f32[2,128,16384]{1,0,2:T(2,128)}), f32[2,128,16384]{1,0,2:T(2,128)}, u32[]{:S(2)}, u32[]{:S(2)}) async-start(f32[2,128,16384]{1,0,2:T(2,128)} %copy.193), calls=%async_computation.3 | async-start | bytes 33554432 | tf_op jit(solution)/shard_map/all_to_all | solution.py:83
  1803.0 4.2 copy-start.4
  1803.0 382.1 %all-to-all-start.4 = ((f32[2,4096,512]{2,0,1:T(2,128)}), f32[2,4096,512]{2,0,1:T(2,128)}, u32[]{:S(2)}, u32[]{:S(2)}) async-start(f32[2,4096,512]{2,0,1:T(2,128)} %copy.199), calls=%async_computation.4 | async-start | bytes 33554432 | tf_op jit(solution)/shard_map/all_to_all | solution.py:87
  2222.9 5.6 collective-permute-start
  2346.9 2.0 copy-start.1
  2346.9 2.0 copy-start.3
where the time goes:
time: 2410 us; the launch traced here: 2390 us
  waiting for transfers between devices  1450 us (60%)
  local copies, waits for them, and re-layouts  460 us (19%)
  matrix products  255 us (11%)
  other arithmetic  204 us (8%)
  starting transfers between devices  24.3 us (1%)
    all_to_all x2, waiting for transfers between devices, spread(): lax.all_to_all(values, ('row', 'col'), split_axis=2, concat_axis=1, tiled...  748 us
    all_to_all x2, waiting for transfers between devices, collect(): lax.all_to_all(values, ('row', 'col'), split_axis=1, concat_axis=2, tiled...  687 us
    sub x8, other arithmetic, complex_product(): real_part = values[0] * cos_part - values[1] * sin_part  128 us
    another operation x2, local copies, waits for them, and re-layouts, complex_product(): return jnp.stack([real_part, imag_part])  94 us
    dot_general x3, matrix products, dft_rows(): jnp.einsum('cbdq,ckbm->dqkm', dft_table(inner_radix, direction), partial_...  81.5 us
    dot_general x3, matrix products, dft_rows(): jnp.einsum('cadk,cabm->dkbm', dft_table(outer_radix, direction), blocked,...  75.5 us
    dot_general x2, matrix products, dft_cols(): jnp.einsum('cbdq,cmkb->dmqk', dft_table(inner_radix, direction), partial_...  63.2 us
    add x1, other arithmetic, local(): weighted + filter_taps[tap_delay][None, :, None] * turned[:, :, offset:of...  50 us
  transfers between devices with their start and end apart: 6, of which 6 were waited for; matrix products, arithmetic and copies ran while one was open for 11% of the time, Pallas kernels for 0%

commit v1 on v0

--- a/solution.py
+++ b/solution.py
@@ -5,6 +5,12 @@
 from jax.sharding import PartitionSpec as P
 
 precise = lax.Precision.HIGHEST
+
+
+def exchange_blocks(shard, mesh_axis, split, join):
+    shards = jnp.split(shard, lax.axis_size(mesh_axis), axis=split)
+    received = lax.all_to_all(jnp.stack(shards), mesh_axis, 0, 0)
+    return jnp.concatenate(received, axis=join)
 
 
 def passed_along(block, axis, distance):
@@ -80,7 +86,7 @@
 
 
 def spread(values):
-    return lax.all_to_all(values, ("row", "col"), split_axis=2, concat_axis=1, tiled=True)
+    return exchange_blocks(values, ("row", "col"), 2, 1)
 
 
 def collect(values):

time: 2410 us -> 2420 us (level)
  local copies, waits for them, and re-layouts: 460 us -> 422 us
  other arithmetic: 204 us -> 229 us
    another operation x2 -> x1, local copies, waits for them, and re-layouts: 94 us -> 32.2 us  [complex_product(): return jnp.stack([real_part, imag_part])]
    all_to_all x2 -> x0, local copies, waits for them, and re-layouts: 40.2 us -> none  [spread(): lax.all_to_all(values, ('row', 'col'), split_axis=2, concat_axis=1, tiled...]
    unnamed x12 -> x50, local copies, waits for them, and re-layouts: 34 us -> 62.3 us
    another operation x0 -> x2, local copies, waits for them, and re-layouts: none -> 26.2 us  [exchange_blocks(): received = lax.all_to_all(jnp.stack(shards), mesh_axis, 0, 0)]
    unnamed x0 -> x31, other arithmetic: none -> 25.6 us
  transfers between devices with their start and end apart: 6 -> 6, of which waited for: 6 -> 6; matrix products, arithmetic and copies ran while one was open for 11% -> 10% of each run, Pallas kernels for 0% -> 0%
where the time goes in v1:
time: 2420 us; the launch traced here: 2410 us
  waiting for transfers between devices  1460 us (60%)
  local copies, waits for them, and re-layouts  422 us (17%)
  matrix products  277 us (11%)
  other arithmetic  229 us (9%)
    all_to_all x2, waiting for transfers between devices, exchange_blocks(): received = lax.all_to_all(jnp.stack(shards), mesh_axis, 0, 0)  748 us
    all_to_all x2, waiting for transfers between devices, collect(): lax.all_to_all(values, ('row', 'col'), split_axis=1, concat_axis=2, tiled...  687 us
    sub x8, other arithmetic, complex_product(): real_part = values[0] * cos_part - values[1] * sin_part  128 us
    dot_general x3, matrix products, dft_rows(): jnp.einsum('cadk,cabm->dkbm', dft_table(outer_radix, direction), blocked,...  97.8 us
    dot_general x3, matrix products, dft_rows(): jnp.einsum('cbdq,ckbm->dqkm', dft_table(inner_radix, direction), partial_...  81.5 us
    dot_general x2, matrix products, dft_cols(): jnp.einsum('cbdq,cmkb->dmqk', dft_table(inner_radix, direction), partial_...  63 us
    unnamed x50, local copies, waits for them, and re-layouts  62.3 us
    add x1, other arithmetic, local(): weighted + filter_taps[tap_delay][None, :, None] * turned[:, :, offset:of...  50 us
  transfers between devices with their start and end apart: 6, of which 6 were waited for; matrix products, arithmetic and copies ran while one was open for 10% of the time, Pallas kernels for 0%

profile of v1, /device:TPU:6, one launch (start us, length us, event | category | flops | bytes accessed | tf_op | source)
XLA Modules:
  0.0 2412.0 jit_solution(8033772466038895484)
XLA Ops:
  0.0 4.8 fusion.208
  4.8 5.1 fusion.207
  9.9 2.2 fusion.145
  12.2 2.2 fusion.144
  38.4 15.2 fusion.123
  64.3 6.1 all-to-all-start
  70.5 9.1 copy.466
  79.5 370.0 %all-to-all-done = f32[32,2,128,512]{3,1,2,0:T(2,128)} async-done(((f32[32,2,128,512]{3,1,2,0:T(2,128)}), f32[32,2,128,512]{3,1,2,0:T(2,128)}, u32[]{:S(2)}, u32[]{:S(2)}) %all-to-all-start) | async-done | bytes 16777248 | tf_op jit(solution)/shard_map/all_to_all | solution.py:12
  449.5 3.4 all-to-all-start.2
  454.0 32.8 %fusion.73 = f32[2,32,128,512]{3,1,2,0:T(8,128)} fusion(f32[32,2,128,512]{3,1,2,0:T(2,128)} %all-to-all-done, f32[1,32,2,32]{1,3,0,2:T(8,128)S(1)} %get-tuple-element.74, f32[1,32,2,32]{1,3,0,2:T(8,128)S(1)} %get-tuple-element.73), kind=kOutput, calls=%fused_computation.170 | convolution fusion | flops 3221229568 | bytes 33570816 | tf_op jit(solution)/shard_map/cadk,cabm->dkbm/dot_general | solution.py:54
  486.8 7.0 multiply_subtract_fusion.5
  493.8 3.3 pad_maximum_fusion
  497.1 28.9 %fusion.61 = f32[2,128,32,512]{3,1,2,0:T(8,128)S(1)} fusion(f32[2,32,128,512]{3,1,2,0:T(8,128)S(1)} %pad_maximum_fusion, f32[1,128,2,128]{1,3,0,2:T(8,128)S(1)} %get-tuple-element.62, f32[1,128,2,128]{1,3,0,2:T(8,128)S(1)} %get-tuple-element.61), kind=kOutput, calls=%fused_computation.166 | convolution fusion | flops 12884967424 | bytes 33816576 | tf_op jit(solution)/shard_map/cbdq,ckbm->dqkm/dot_general | solution.py:59
  526.0 7.0 fusion.206
  533.0 8.2 copy.457
  541.3 8.2 copy.458
  549.5 36.9 %fusion.53 = (f32[1,4096,512]{2,1,0:T(8,128)S(1)}, f32[1,4096,512]{2,1,0:T(8,128)S(1)}) fusion(f32[1,128,32,512]{3,2,1,0:T(8,128)S(1)} %copy.458, f32[1,128,32,512]{3,2,1,0:T(8,128)S(1)} %copy.457, s32[512]{0:T(512)S(1)} %iota_add_fusion), kind=kLoop, calls=%fused_computation.140 | loop fusion | flops 41943040 | bytes 33556480 | tf_op jit(solution)/shard_map/sub | solution.py:34
  586.4 1.8 pad_maximum_fusion.1
  588.3 32.2 %copy.459 = f32[2,4096,512]{2,0,1:T(2,128)} copy(f32[2,4096,512]{2,1,0:T(8,128)S(1)} %pad_maximum_fusion.1) | data formatting | bytes 33554432 | tf_op jit(solution)/shard_map/stack | solution.py:36
  620.5 20.7 all-to-all-done.2
  641.2 5.2 all-to-all-start.1
  647.5 31.6 %sine_bitcast_fusion = (f32[128,32,512]{2,0,1:T(8,128)}, f32[128,32,512]{2,0,1:T(8,128)}) fusion(f32[32,128,512]{2,1,0:T(8,128)} %all-to-all-done.2), kind=kLoop, calls=%fused_computation.156 | loop fusion | bytes 25165824 | tf_op jit(solution)/shard_map/sin | solution.py:115
  679.1 9.0 copy.467
  688.1 9.4 copy.468
  697.5 8.9 copy.469
  706.4 9.4 copy.470
  715.8 309.3 %all-to-all-done.1 = f32[2,4096,512]{2,0,1:T(2,128)} async-done(((f32[2,4096,512]{2,0,1:T(2,128)}), f32[2,4096,512]{2,0,1:T(2,128)}, u32[]{:S(2)}, u32[]{:S(2)}) %all-to-all-start.1) | async-done | bytes 16777248 | tf_op jit(solution)/shard_map/all_to_all | solution.py:93
  1025.2 14.2 copy.460
  1039.3 17.5 copy.461
  1056.8 18.1 copy.496
  1074.9 17.1 convolution_bitcast_fusion
  1092.0 7.0 multiply_subtract_fusion.4
  1099.0 31.3 %fusion.38 = f32[2,128,128,128]{2,3,0,1:T(8,128)} fusion(f32[1,128,128,128]{2,3,0,1:T(8,128)} %get-tuple-element.14, f32[1,128,128,128]{2,3,0,1:T(8,128)} %get-tuple-element.13, f32[1,128,2,128]{1,3,0,2:T(8,128)S(1)} %get-tuple-element.62, f32[1,128,2,128]{1,3,0,2:T(8,128)S(1)} %get-tuple-element.61), kind=kOutput, calls=%fused_computation.122 | convolution fusion | flops 12889161728 | bytes 33816576 | tf_op jit(solution)/shard_map/cbdq,cmkb->dmqk/dot_general | solution.py:76
  1130.3 18.9 multiply_subtract_fusion.3
  1149.2 17.6 fusion.39
  1166.8 7.1 multiply_subtract_fusion.2
  1173.9 31.7 %fusion.42 = f32[2,128,128,128]{2,3,0,1:T(8,128)S(1)} fusion(f32[1,128,128,128]{2,3,0,1:T(8,128)} %get-tuple-element.12, f32[1,128,128,128]{2,3,0,1:T(8,128)} %get-tuple-element.11, f32[1,128,2,128]{1,3,2,0:T(8,128)S(1)} %get-tuple-element.60, f32[1,128,2,128]{1,3,2,0:T(8,128)S(1)} %get-tuple-element.59), kind=kOutput, calls=%fused_computation.124 | convolution fusion | flops 12889161728 | bytes 33816576 | tf_op jit(solution)/shard_map/cbdq,cmkb->dmqk/dot_general | solution.py:76
  1205.6 6.7 fusion.205
  1212.3 9.4 copy.476
  1221.7 9.3 copy.477
  1231.0 36.6 %fusion.51 = (f32[1,128,16384]{1,2,0:T(8,128)S(1)}, f32[1,128,16384]{1,2,0:T(8,128)S(1)}) fusion(f32[1,128,128,128]{1,3,2,0:T(8,128)} %copy.477, f32[1,128,128,128]{1,3,2,0:T(8,128)} %copy.476, s32[128]{0:T(128)S(1)} %iota_add_fusion.1), kind=kLoop, calls=%fused_computation.134 | loop fusion | flops 46137344 | bytes 33554944 | tf_op jit(solution)/shard_map/sub | solution.py:34
  1294.1 25.0 %copy.478 = f32[32,2,128,512]{3,1,2,0:T(2,128)} copy(f32[32,2,128,512]{2,3,1,0:T(8,128)} %fusion.113) | data formatting | bytes 33554432 | tf_op jit(solution)/shard_map/stack | solution.py:12
  1319.0 3.6 all-to-all-start.3
  1323.1 378.0 %all-to-all-done.3 = f32[32,2,128,512]{3,1,2,0:T(2,128)} async-done(((f32[32,2,128,512]{3,1,2,0:T(2,128)}), f32[32,2,128,512]{3,1,2,0:T(2,128)}, u32[]{:S(2)}, u32[]{:S(2)}) %all-to-all-start.3) | async-done | bytes 16777248 | tf_op jit(solution)/shard_map/all_to_all | solution.py:12
  1701.2 32.7 %fusion.76 = f32[2,32,128,512]{3,1,2,0:T(8,128)} fusion(f32[32,2,128,512]{3,1,2,0:T(2,128)} %all-to-all-done.3, f32[1,32,2,32]{1,3,2,0:T(8,128)S(1)} %get-tuple-element.72, f32[1,32,2,32]{1,3,2,0:T(8,128)S(1)} %get-tuple-element.71), kind=kOutput, calls=%fused_computation.171 | convolution fusion | flops 3221229568 | bytes 33570816 | tf_op jit(solution)/shard_map/cadk,cabm->dkbm/dot_general | solution.py:54
  1733.9 7.0 multiply_subtract_fusion.1
  1740.9 3.3 pad_maximum_fusion.2
  1744.2 28.9 %fusion.64 = f32[2,128,32,512]{3,1,2,0:T(8,128)S(1)} fusion(f32[2,32,128,512]{3,1,2,0:T(8,128)S(1)} %pad_maximum_fusion.2, f32[1,128,2,128]{1,3,2,0:T(8,128)S(1)} %copy-done.7, f32[1,128,2,128]{1,3,2,0:T(8,128)S(1)} %copy-done.5), kind=kOutput, calls=%fused_computation.167 | convolution fusion | flops 12884967424 | bytes 33816576 | tf_op jit(solution)/shard_map/cbdq,ckbm->dqkm/dot_general | solution.py:59
  1773.1 20.1 copy.483
  1793.2 28.6 %copy.484 = f32[2,4096,512]{2,0,1:T(2,128)} copy(f32[2,4096,512]{2,1,0:T(8,128)} %bitcast.421) | data formatting | bytes 33554432 | tf_op jit(solution)/shard_map/reshape | solution.py:62
  1821.8 3.8 all-to-all-start.4
  1826.0 377.8 %all-to-all-done.4 = f32[2,4096,512]{2,0,1:T(2,128)} async-done(((f32[2,4096,512]{2,0,1:T(2,128)}), f32[2,4096,512]{2,0,1:T(2,128)}, u32[]{:S(2)}, u32[]{:S(2)}) %all-to-all-start.4) | async-done | bytes 16777248 | tf_op jit(solution)/shard_map/all_to_all | solution.py:93
  2203.8 17.8 copy.702
  2221.6 19.2 reshape_reshape.3
  2241.7 1.9 collective-permute-start
  2243.7 3.5 collective-permute-done
  2247.2 11.8 maximum_bitcast_fusion
  2259.1 50.0 %fusion = f32[2,1024,2048]{1,2,0:T(8,128)} fusion(f32[2,1024,2055]{1,2,0:T(8,128)} %maximum_bitcast_fusion, f32[1024]{0:T(1024)S(1)} %bitcast.433, f32[1024]{0:T(1024)S(1)} %bitcast.434, f32[1024]{0:T(1024)S(1)} %bitcast.428, f32[1024]{0:T(1024)S(1)} %bitcast.429, f32[1024]{0:T(1024)S(1)} %bitcast.430, f32[1024]{0:T(1024)S(1)} %bitcast.431, ...), kind=kLoop, calls=%fused_computation.64 | loop fusion | flops 62914560 | bytes 151027712 | tf_op jit(solution)/shard_map/add | solution.py:135
  2309.1 17.3 copy.486
  2326.4 32.2 %fusion.67 = f32[2,8,128,2048]{3,1,2,0:T(8,128)} fusion(f32[2,8,128,2048]{3,2,1,0:T(8,128)} %bitcast.423, f32[1,8,2,8]{1,3,0,2:T(8,128)S(1)} %copy.421, f32[1,8,2,8]{1,3,0,2:T(8,128)S(1)} %copy.420), kind=kOutput, calls=%fused_computation.168 | convolution fusion | flops 805306624 | bytes 33555456 | tf_op jit(solution)/shard_map/cadk,cabm->dkbm/dot_general | solution.py:54
  2358.6 7.2 multiply_subtract_fusion
  2365.9 2.0 pad_maximum_fusion.3
  2367.9 23.7 fusion.70
  2391.6 20.2 copy.701
  (108 shorter events, 65.2 us)
Async XLA Ops:
  64.3 385.2 %all-to-all-start = ((f32[32,2,128,512]{3,1,2,0:T(2,128)}), f32[32,2,128,512]{3,1,2,0:T(2,128)}, u32[]{:S(2)}, u32[]{:S(2)}) async-start(f32[32,2,128,512]{3,1,2,0:T(2,128)} %fusion.114), calls=%async_computation | async-start | bytes 33554432 | tf_op jit(solution)/shard_map/all_to_all | solution.py:12
  449.5 191.7 %all-to-all-start.2 = ((f32[32,128,512]{2,1,0:T(8,128)}), f32[32,128,512]{2,1,0:T(8,128)}, u32[]{:S(2)}, u32[]{:S(2)}) async-start(f32[32,128,512]{2,1,0:T(8,128)} %bitcast.424), calls=%async_computation.2 | async-start | bytes 16777216 | tf_op jit(solution)/shard_map/all_to_all | solution.py:112
  454.0 645.0 %copy-start = (f32[1,128,2,128]{1,3,0,2:T(8,128)}, f32[1,128,2,128]{1,3,0,2:T(8,128)S(1)}, u32[]{:S(2)}) copy-start(f32[1,128,2,128]{1,3,0,2:T(8,128)S(1)} %get-tuple-element.61) | copy-start | bytes 393220
  454.0 645.0 %copy-start.2 = (f32[1,128,2,128]{1,3,0,2:T(8,128)}, f32[1,128,2,128]{1,3,0,2:T(8,128)S(1)}, u32[]{:S(2)}) copy-start(f32[1,128,2,128]{1,3,0,2:T(8,128)S(1)} %get-tuple-element.62) | copy-start | bytes 393220
  641.2 384.0 %all-to-all-start.1 = ((f32[2,4096,512]{2,0,1:T(2,128)}), f32[2,4096,512]{2,0,1:T(2,128)}, u32[]{:S(2)}, u32[]{:S(2)}) async-start(f32[2,4096,512]{2,0,1:T(2,128)} %copy.459), calls=%async_computation.1 | async-start | bytes 33554432 | tf_op jit(solution)/shard_map/all_to_all | solution.py:93
  647.5 526.4 %copy-start.4 = (f32[1,128,2,128]{1,3,2,0:T(8,128)}, f32[1,128,2,128]{1,3,2,0:T(8,128)S(1)}, u32[]{:S(2)}) copy-start(f32[1,128,2,128]{1,3,2,0:T(8,128)S(1)} %get-tuple-element.59) | copy-start | bytes 393220
  647.5 526.4 %copy-start.6 = (f32[1,128,2,128]{1,3,2,0:T(8,128)}, f32[1,128,2,128]{1,3,2,0:T(8,128)S(1)}, u32[]{:S(2)}) copy-start(f32[1,128,2,128]{1,3,2,0:T(8,128)S(1)} %get-tuple-element.60) | copy-start | bytes 393220
  1319.0 382.1 %all-to-all-start.3 = ((f32[32,2,128,512]{3,1,2,0:T(2,128)}), f32[32,2,128,512]{3,1,2,0:T(2,128)}, u32[]{:S(2)}, u32[]{:S(2)}) async-start(f32[32,2,128,512]{3,1,2,0:T(2,128)} %copy.478), calls=%async_computation.3 | async-start | bytes 33554432 | tf_op jit(solution)/shard_map/all_to_all | solution.py:12
  1740.9 3.3 copy-start.5
  1740.9 3.3 copy-start.7
  1821.8 4.2 copy-start.8
  1821.8 382.1 %all-to-all-start.4 = ((f32[2,4096,512]{2,0,1:T(2,128)}), f32[2,4096,512]{2,0,1:T(2,128)}, u32[]{:S(2)}, u32[]{:S(2)}) async-start(f32[2,4096,512]{2,0,1:T(2,128)} %copy.484), calls=%async_computation.4 | async-start | bytes 33554432 | tf_op jit(solution)/shard_map/all_to_all | solution.py:93
  2241.7 5.6 collective-permute-start
  2365.9 2.0 copy-start.1
  2365.9 2.0 copy-start.3
